TPU v7x, 512 devices: a whole 4x8x8 slice. The times are simulated.
512 devices in a mesh: dp: 8 (over z), fsdp: 64 (over y, x, core).
Axes of the slice: x: 4, y: 8, z: 8, core: 2. Of those that a mesh axis runs over, the one named last changes fastest.
Arguments:
- small_cols: bfloat16 [393216, 128], P(('dp', 'fsdp')), may hold values from -24 to 24
- wide_cols: bfloat16 [393216, 2, 1536], P(('dp', 'fsdp')), may hold values from -24 to 24
- token_counts: int32 [512], P(('dp', 'fsdp')), may hold values from 144 to 768, as said below
- loss_sums: float32 [512], P(('dp', 'fsdp'))
- weight: float32 [128, 1536], P('fsdp'), may hold values from -0.75 to 0.75
- first_moment: float32 [128, 1536], P('fsdp'), may hold values from -0.002 to 0.002
- second_moment: float32 [128, 1536], P('fsdp'), may hold values from 1e-07 to 1e-06
- step: int32 [], replicated, may hold values from 1 to 2999
Outputs:
- new_weight: float32 [128, 1536], P('fsdp')
- new_first: float32 [128, 1536], P('fsdp')
- new_second: float32 [128, 1536], P('fsdp')
- adam_step: float32 [128, 1536], P('fsdp')
- grad_norm: float32 [], replicated
- mean_loss: float32 [], replicated
Inputs may be any that keep to these rules, and one draw needn't show every extreme that they name: `token_counts`: each count is f * h * w with f from 1 to 3 and h, w from 12 to 16; in every draw some device's count is exactly 768.
All inputs are finite; a program needn't handle non-finite values.
Results may differ from a plain program's by a relative error of at most 0.0003.
Values sent between devices are 32-bit elements; how exact they have to be, the bound alone decides.
A program may use at most 64 MiB of HBM per device.

v0:
```python
import jax
import jax.numpy as jnp
from jax import lax
from jax.sharding import PartitionSpec as P

MAX_NORM = 1.0
BETA_FIRST = 0.9
BETA_SECOND = 0.999
EPSILON_ADAM = 1e-08
LEARN_RATE = 0.02
DECAY_RATE = 0.1


def in_blocks(array, dim, peers):
    lengths = array.shape
    parts = array.reshape(*lengths[:dim], peers, lengths[dim] // peers, *lengths[dim + 1 :])
    return jnp.moveaxis(parts, dim, 0)


def sum_at_owner(array, axis, dim):
    peers = lax.axis_size(axis)
    parts = lax.all_to_all(in_blocks(array, dim, peers), axis, 0, 0, tiled=True)
    return jnp.sum(parts, axis=0)


def from_everyone(array, axis):
    peers = lax.axis_size(axis)
    return lax.all_to_all(
        jnp.broadcast_to(array[None], (peers, *array.shape)), axis, 0, 0, tiled=True
    )


def taken_together(array, axis):
    everything = from_everyone(array, axis)
    return jnp.sum(everything, axis=0)


def in_one(arrays, axis):
    ends = [0]
    for a in arrays:
        ends.append(ends[-1] + a.size)
    total = taken_together(jnp.concatenate([a.ravel() for a in arrays]), axis)
    return tuple((total[b:e].reshape(a.shape) for a, b, e in zip(arrays, ends, ends[1:])))


def slot_product(narrow, broad, live_count):
    block_rows = narrow.shape[0]
    half_cols = narrow.shape[1] // 2
    is_live = jnp.arange(block_rows, dtype=jnp.int32) < live_count
    narrow = jnp.where(is_live[:, None], narrow, jnp.zeros_like(narrow))
    portion = jnp.einsum(
        "thc,thd->hcd",
        narrow.reshape(block_rows, 2, half_cols),
        broad,
        preferred_element_type=jnp.float32,
    )
    return portion.reshape(2 * half_cols, broad.shape[2])


def device_term(small_cols, wide_cols, live_count):
    return slot_product(small_cols, wide_cols, live_count)


def on_device(
    small_cols, wide_cols, token_counts, loss_sums, weight, first_moment, second_moment, step
):
    live_count = token_counts[0]
    contribution = device_term(small_cols, wide_cols, live_count)
    count_float = token_counts.astype(jnp.float32)[0]
    loss_local = loss_sums[0]
    owned_sum = sum_at_owner(contribution, "fsdp", 0)
    summed, count_groups, loss_groups = in_one((owned_sum, count_float, loss_local), "dp")
    squares, token_total, loss_total = in_one(
        (jnp.sum(summed * summed), count_groups, loss_groups), "fsdp"
    )
    gradient = summed / token_total
    grad_norm = jnp.sqrt(squares) / token_total
    mean_loss = loss_total / token_total
    clip_factor = jnp.minimum(1.0, MAX_NORM / (grad_norm + 1e-06))
    clipped = gradient * clip_factor
    new_first = BETA_FIRST * first_moment + (1.0 - BETA_FIRST) * clipped
    new_second = BETA_SECOND * second_moment + (1.0 - BETA_SECOND) * clipped * clipped
    step_float = step.astype(jnp.float32)
    first_hat = new_first / (1.0 - jnp.power(jnp.float32(BETA_FIRST), step_float))
    second_hat = new_second / (1.0 - jnp.power(jnp.float32(BETA_SECOND), step_float))
    adam_step = first_hat / (jnp.sqrt(second_hat) + EPSILON_ADAM) + DECAY_RATE * weight
    new_weight = weight - LEARN_RATE * adam_step
    return (new_weight, new_first, new_second, adam_step, grad_norm, mean_loss)


def solution(mesh):
    in_specs = (
        P(("dp", "fsdp"), None),
        P(("dp", "fsdp"), None, None),
        P(("dp", "fsdp")),
        P(("dp", "fsdp")),
        P("fsdp", None),
        P("fsdp", None),
        P("fsdp", None),
        P(),
    )
    out_specs = (P("fsdp", None), P("fsdp", None), P("fsdp", None), P("fsdp", None), P(), P())
    return jax.shard_map(
        on_device, mesh=mesh, in_specs=in_specs, out_specs=out_specs, check_vma=False
    )
```

profile of v0, /device:TPU:1, one launch (start us, length us, event | category | flops | bytes accessed | tf_op | source)
XLA Modules:
  0.0 85.4 jit_solution(13052749407866836515)
XLA Ops:
  1.3 1.1 %copy.24 = bf16[768,128]{0,1:T(8,128)(2,1)S(1)} copy(bf16[768,128]{1,0:T(8,128)(2,1)} %param.8) | data formatting | bytes 393216 | tf_op args[0]
  2.4 0.0 copy-start
  2.4 0.0 copy-start.1
  2.4 0.0 copy-start.2
  2.4 3.3 %fusion = f32[2,64,1536]{2,1,0:T(8,128)S(1)} fusion(bf16[768,2,64]{0,2,1:T(8,128)(2,1)S(1)} %bitcast.8, bf16[768,2,1536]{2,1,0:T(2,128)(2,1)} %param.9), kind=kOutput, calls=%fused_computation | convolution fusion | flops 301989888 | bytes 5701632 | tf_op jit(solution)/shard_map/thc,thd->hcd/dot_general | solution.py:51
  5.7 1.3 %reshape_reshape.3 = f32[64,2,1536]{2,1,0:T(2,128)} reshape(f32[2,64,1536]{2,1,0:T(8,128)S(1)} %fusion) | data formatting | bytes 1572864 | tf_op jit(solution)/shard_map/reshape;reshape | solution.py:16
  7.0 11.6 %all-to-all-start = ((f32[64,2,1536]{2,1,0:T(2,128)}), f32[64,2,1536]{2,1,0:T(2,128)S(1)}, u32[]{:S(2)}, u32[]{:S(2)}) async-start(f32[64,2,1536]{2,1,0:T(2,128)} %reshape_reshape.3), calls=%async_computation | async-start | bytes 1572864 | tf_op jit(solution)/shard_map/all_to_all | solution.py:22
  19.3 22.4 %all-to-all-done = f32[64,2,1536]{2,1,0:T(2,128)S(1)} async-done(((f32[64,2,1536]{2,1,0:T(2,128)}), f32[64,2,1536]{2,1,0:T(2,128)S(1)}, u32[]{:S(2)}, u32[]{:S(2)}) %all-to-all-start) | async-done | bytes 786464 | tf_op jit(solution)/shard_map/all_to_all | solution.py:22
  41.7 0.3 reduce_sum.36
  41.9 0.1 concatenate.7
  42.0 0.1 broadcast_in_dim.26
  42.1 17.5 %all_to_all.17 = f32[8,1,3074]{2,1,0:T(1,128)S(1)} all-to-all(f32[8,1,3074]{2,1,0:T(1,128)S(1)} %broadcast_in_dim.26), channel_id=1, replica_groups=mesh['dp'=8,'fsdp'=64] {'dp'}, dimensions={0} | all-to-all | bytes 196736 | tf_op jit(solution)/shard_map/all_to_all | solution.py:28
  59.6 0.1 reduce_sum.37
  59.6 0.6 multiply_reduce_fusion
  60.3 0.7 pad_maximum_fusion
  61.0 0.6 broadcast_in_dim.27
  61.6 7.3 %all-to-all-start.2 = ((f32[64,1,3]{2,1,0:T(1,128)}), f32[64,1,3]{2,1,0:T(1,128)S(1)}, u32[]{:S(2)}, u32[]{:S(2)}) async-start(f32[64,1,3]{2,1,0:T(1,128)} %broadcast_in_dim.27), calls=%async_computation.2 | async-start | bytes 65536 | tf_op jit(solution)/shard_map/all_to_all | solution.py:28
  69.6 8.7 %all-to-all-done.2 = f32[64,1,3]{2,1,0:T(1,128)S(1)} async-done(((f32[64,1,3]{2,1,0:T(1,128)}), f32[64,1,3]{2,1,0:T(1,128)S(1)}, u32[]{:S(2)}, u32[]{:S(2)}) %all-to-all-start.2) | async-done | bytes 800 | tf_op jit(solution)/shard_map/all_to_all | solution.py:28
  78.3 0.1 reduce_sum.39
  78.4 0.6 fusion.4
  80.4 0.7 divide_multiply_fusion
  82.4 0.0 copy-done
  82.4 0.0 copy-done.1
  82.4 0.0 copy-done.2
  82.5 0.7 multiply_subtract_fusion
  (5 shorter events, 0.1 us)
Async XLA Ops:
  2.4 80.0 %copy-start = (f32[2,1536]{1,0:T(2,128)S(1)}, f32[2,1536]{1,0:T(2,128)}, u32[]{:S(2)}) copy-start(f32[2,1536]{1,0:T(2,128)} %param.12) | copy-start | bytes 36868
  2.4 80.0 %copy-start.1 = (f32[2,1536]{1,0:T(2,128)S(1)}, f32[2,1536]{1,0:T(2,128)}, u32[]{:S(2)}) copy-start(f32[2,1536]{1,0:T(2,128)} %param.14) | copy-start | bytes 36868
  2.4 80.0 %copy-start.2 = (f32[2,1536]{1,0:T(2,128)S(1)}, f32[2,1536]{1,0:T(2,128)}, u32[]{:S(2)}) copy-start(f32[2,1536]{1,0:T(2,128)} %param.13) | copy-start | bytes 36868
  7.0 34.6 %all-to-all-start = ((f32[64,2,1536]{2,1,0:T(2,128)}), f32[64,2,1536]{2,1,0:T(2,128)S(1)}, u32[]{:S(2)}, u32[]{:S(2)}) async-start(f32[64,2,1536]{2,1,0:T(2,128)} %reshape_reshape.3), calls=%async_computation | async-start | bytes 1572864 | tf_op jit(solution)/shard_map/all_to_all | solution.py:22
  61.6 16.7 %all-to-all-start.2 = ((f32[64,1,3]{2,1,0:T(1,128)}), f32[64,1,3]{2,1,0:T(1,128)S(1)}, u32[]{:S(2)}, u32[]{:S(2)}) async-start(f32[64,1,3]{2,1,0:T(1,128)} %broadcast_in_dim.27), calls=%async_computation.2 | async-start | bytes 65536 | tf_op jit(solution)/shard_map/all_to_all | solution.py:28
where the time goes:
time: 85.8 us; the launch traced here: 85.4 us
  waiting for transfers between devices  31 us (36%)
  starting transfers between devices  18.9 us (22%)
  blocking collectives  17.5 us (20%)
  between operations  7.79 us (9%)
  local copies, waits for them, and re-layouts  3.8 us (4%)
  matrix products  3.28 us (4%)
  other arithmetic  3.08 us (4%)
    all_to_all x1, waiting for transfers between devices, sum_at_owner(): parts = lax.all_to_all(in_blocks(array, dim, peers), axis, 0, 0, tiled=True)  22.4 us
    all_to_all x1, blocking collectives, from_everyone(): lax.all_to_all(jnp.broadcast_to(array[None], (peers, *array.shape)), axis...  17.5 us
    all_to_all x1, starting transfers between devices, sum_at_owner(): parts = lax.all_to_all(in_blocks(array, dim, peers), axis, 0, 0, tiled=True)  11.6 us
    all_to_all x1, waiting for transfers between devices, from_everyone(): lax.all_to_all(jnp.broadcast_to(array[None], (peers, *array.shape)), axis...  8.67 us
    all_to_all x1, starting transfers between devices, from_everyone(): lax.all_to_all(jnp.broadcast_to(array[None], (peers, *array.shape)), axis...  7.31 us
    dot_general x1, matrix products, slot_product(): jnp.einsum('thc,thd->hcd', narrow.reshape(block_rows, 2, half_cols), broa...  3.28 us
  transfers between devices with their start and end apart: 2, of which 2 were waited for; matrix products, arithmetic and copies ran while one was open for 0% of the time, Pallas kernels for 0%

commit v1 on v0

v1 whole, which is shorter than its diff:
```python
import functools
import math

import jax
import jax.numpy as jnp
import numpy as np
from jax import lax
from jax.experimental import pallas as pl
from jax.experimental.pallas import tpu as pltpu
from jax.sharding import PartitionSpec as P

MAX_NORM = 1.0
BETA_FIRST = 0.9
BETA_SECOND = 0.999
EPSILON_ADAM = 1e-08
LEARN_RATE = 0.02
DECAY_RATE = 0.1

MESH = pl.DeviceIdType.MESH
F32 = jnp.float32
BF16 = jnp.bfloat16
TOKENS, ROWS, WIDTH = 768, 128, 1536
TILES = WIDTH // 128
CHUNKS = 6
GROUPS = 3
X, Y, Z = 4, 8, 8
PLANE = 64


def iota(shape, dim):
    return lax.broadcasted_iota(jnp.int32, shape, dim)


def one_minus_power(beta, step):
    u = step * F32(math.log(float(np.float32(beta))))
    series = jnp.ones_like(u)
    for n in range(10, 1, -1):
        series = 1.0 + u * series * F32(1.0 / n)
    return jnp.where(u > -0.5, -u * series, 1.0 - jnp.exp(u))


def left_operand(small, count, left):
    row, col = iota((128, 128), 0), iota((128, 128), 1)
    core, x, r, y = row >> 6, (row >> 4) & 3, (row >> 3) & 1, row & 7
    order = (col == y * 16 + x * 4 + core * 2 + r).astype(F32).astype(BF16)
    second = y >= 4
    spread_row, spread_col = iota((256, 256), 0), iota((256, 256), 1)
    spread = (spread_col == ((spread_row & 127) << 1) + (spread_row >> 7)).astype(F32).astype(BF16)
    for b in range(TOKENS // 128):
        block = small[pl.ds(b * 128, 128), :].astype(F32)
        block = jnp.where(row + b * 128 < count, block, 0.0).astype(BF16)
        turned = lax.dot_general(order, block, (((1,), (1,)), ((), ())), preferred_element_type=F32)
        halves = jnp.concatenate(
            [jnp.where(second, 0.0, turned), jnp.where(second, turned, 0.0)], axis=1
        ).astype(BF16)
        left[:, pl.ds(b * 256, 256)] = jnp.dot(halves, spread, preferred_element_type=F32).astype(BF16)


def kernel(
    small_hbm, wide_hbm, count_hbm, loss_hbm, weight_hbm, first_hbm, second_hbm, step_hbm,
    new_weight, new_first, new_second, adam, scalars,
    small, wide, left, part, core_in, held, opposite_in, direct_in, merged, merged_in, lines, y_in, y_sum,
    z_in, pair, pair_in, note, notes_in, states, count_smem, loss_smem, step_smem,
    load_sem, wide_sem, smem_sem, core_send, core_recv, opp_send, opp_recv, dir_send, dir_recv, mer_send, mer_recv,
    y_send, y_recv, z_send, z_recv, pair_send, pair_recv, note_send, note_recv, relay,
):
    z, f = lax.axis_index("dp"), lax.axis_index("fsdp")
    c, x, y = lax.rem(f, 2), lax.rem(lax.div(f, 2), X), lax.div(f, 2 * X)

    def at(z_, y_, x_, c_):
        return (z_, (y_ * X + x_) * 2 + c_)

    x_up, x_down, x_far = lax.rem(x + 1, X), lax.rem(x + X - 1, X), lax.rem(x + 2, X)
    y_up, y_down = lax.rem(y + 1, Y), lax.rem(y + Y - 1, Y)
    z_up, z_down = lax.rem(z + 1, Z), lax.rem(z + Z - 1, Z)
    partner = at(z, y, x, 1 - c)
    to_x_up, to_x_down = at(z, y, x_up, c), at(z, y, x_down, c)
    ring = (at(z, y_up, x, c), at(z, y_down, x, c), at(z_up, y, x, c), at(z_down, y, x, c))

    barrier = pltpu.get_barrier_semaphore()
    for device in (partner, to_x_up, to_x_down) + ring:
        pl.semaphore_signal(barrier, inc=1, device_id=device, device_id_type=MESH)

    loads = [pltpu.make_async_copy(small_hbm, small, load_sem.at[0])]
    smem_loads = [
        pltpu.make_async_copy(count_hbm, count_smem, smem_sem.at[0]),
        pltpu.make_async_copy(loss_hbm, loss_smem, smem_sem.at[1]),
        pltpu.make_async_copy(step_hbm, step_smem, smem_sem.at[2]),
    ]
    columns = [
        pltpu.make_async_copy(wide_hbm.at[:, :, pl.ds(t * 128, 128)], wide.at[t], wide_sem.at[t])
        for t in range(TILES)
    ]
    for n, array in enumerate((weight_hbm, first_hbm, second_hbm)):
        loads.append(pltpu.make_async_copy(array, states.at[n], load_sem.at[n + 1]))
    for copy in loads[:1] + smem_loads + columns + loads[1:]:
        copy.start()

    def remote(src, dst, send, recv, device):
        copy = pltpu.make_async_remote_copy(
            src_ref=src, dst_ref=dst, send_sem=send, recv_sem=recv, device_id=device, device_id_type=MESH
        )
        copy.start()
        return copy

    def wait_bytes(ref, sem):
        pltpu.make_async_copy(ref, ref, sem).wait()

    def relay_signal(n):
        for device in ring:
            pl.semaphore_signal(relay.at[n], inc=1, device_id=device, device_id_type=MESH)

    for copy in smem_loads[:2]:
        copy.wait()
    loads[0].wait()
    left_operand(small, count_smem[0], left)

    to_core, to_opp, to_dir, to_mer = {}, {}, {}, {}

    def multiply(k):
        columns[2 * k].wait()
        columns[2 * k + 1].wait()
        right = jnp.concatenate([wide[2 * k + n].reshape(2 * TOKENS, 128) for n in range(2)], axis=1)
        product = jnp.dot(left[...], right, preferred_element_type=F32)
        part[k] = product.reshape(2, X, 16, 256)

    def core_out(k):
        to_core[k] = remote(part.at[k, 1 - c], core_in.at[k], core_send.at[k], core_recv.at[k], partner)

    def core_add(k):
        to_core[k].wait_recv()
        held[k] = part[k, c] + core_in[k]
        near, far = (to_x_up, to_x_down) if k % 2 == 0 else (to_x_down, to_x_up)
        to_opp[k] = remote(held.at[k, x_far], opposite_in.at[k], opp_send.at[k], opp_recv.at[k], near)
        other = x_down if k % 2 == 0 else x_up
        to_dir[k] = remote(held.at[k, other], direct_in.at[k], dir_send.at[k], dir_recv.at[k], far)

    def x_merge(k):
        to_opp[k].wait_recv()
        near, index = (to_x_up, x_up) if k % 2 == 0 else (to_x_down, x_down)
        merged[k] = held[k, index] + opposite_in[k]
        to_mer[k] = remote(merged.at[k], merged_in.at[k], mer_send.at[k], mer_recv.at[k], near)

    def x_final(k):
        to_dir[k].wait_recv()
        to_mer[k].wait_recv()
        total = held[k, x] + direct_in[k] + merged_in[k]
        g, half = k // 2, k % 2
        for r in range(2):
            for t in range(2):
                lines[g, pl.ds(2 * (2 * half + t) + r, 8, stride=8), :] = total[8 * r : 8 * r + 8, 128 * t : 128 * t + 128]

    def y_out(g):
        for d in range(1, Y):
            to = lax.rem(y + d, Y)
            remote(
                lines.at[g, pl.ds(pl.multiple_of(to * 8, 8), 8)], y_in.at[g, d - 1],
                y_send.at[g], y_recv.at[g], at(z, to, x, c),
            )

    def y_add(g):
        wait_bytes(y_in.at[g], y_recv.at[g])
        total = lines[g, pl.ds(pl.multiple_of(y * 8, 8), 8), :]
        for d in range(Y - 1):
            total = total + y_in[g, d]
        y_sum[g] = total
        z_in[g, z] = total
        for d in range(1, Z):
            to = lax.rem(z + d, Z)
            remote(y_sum.at[g], z_in.at[g, z], z_send.at[g], z_recv.at[g], at(to, y, x, c))

    multiply(0)
    pl.semaphore_wait(barrier, 7)
    core_out(0)
    relay_signal(0)
    multiply(1)
    core_out(1)
    multiply(2)
    core_out(2)
    core_add(0)
    pl.semaphore_wait(relay.at[0], 4)
    relay_signal(1)
    multiply(3)
    core_out(3)
    core_add(1)
    multiply(4)
    core_out(4)
    core_add(2)
    pl.semaphore_wait(relay.at[1], 4)
    relay_signal(2)
    multiply(5)
    core_out(5)
    core_add(3)
    core_add(4)
    x_merge(0)
    core_add(5)
    x_merge(1)
    pl.semaphore_wait(relay.at[2], 4)

    lane = iota((1, 128), 1)
    mine = jnp.where(
        lane == 64, count_smem[0].astype(F32), jnp.where(lane == 65, loss_smem[0], 0.0)
    )
    pair[...] = mine
    pair_in[z] = mine
    for d in range(1, Z):
        remote(pair, pair_in.at[z], pair_send, pair_recv, at(lax.rem(z + d, Z), y, x, c))

    x_merge(2)
    x_final(0)
    x_merge(3)
    x_final(1)
    y_out(0)
    x_merge(4)
    x_final(2)
    x_merge(5)
    x_final(3)
    y_out(1)
    x_final(4)
    x_final(5)
    y_out(2)

    for g in range(GROUPS):
        y_add(g)
    totals = []
    squares = jnp.zeros((8, 128), F32)
    for g in range(GROUPS):
        wait_bytes(z_in.at[g, pl.ds(0, Z - 1)], z_recv.at[g])
        total = z_in[g, 0]
        for n in range(1, Z):
            total = total + z_in[g, n]
        totals.append(total)
        squares = squares + total * total
    wait_bytes(pair_in.at[pl.ds(0, Z - 1)], pair_recv)
    pairs = pair_in[0]
    for n in range(1, Z):
        pairs = pairs + pair_in[n]
    squares = jnp.sum(squares, axis=0, keepdims=True)
    squares = squares + pltpu.roll(squares, 64, 1)
    mine = jnp.where(lane < 64, squares, pairs)
    note[...] = mine
    notes_in[f] = mine
    for d in range(1, PLANE):
        to = lax.rem(f + d, PLANE)
        remote(note, notes_in.at[f], note_send, note_recv, (z, to))

    for copy in loads[1:] + smem_loads[2:]:
        copy.wait()
    step = jnp.full((8, 128), step_smem[0].astype(F32), F32)
    first_scale = 1.0 / one_minus_power(BETA_FIRST, step)
    second_scale = 1.0 / one_minus_power(BETA_SECOND, step)

    wait_bytes(notes_in.at[pl.ds(0, PLANE - 1)], note_recv)
    everything = jnp.sum(notes_in[...].reshape(PLANE, 128), axis=0, keepdims=True)
    square_total = jnp.sum(jnp.where(lane < 64, everything, 0.0), axis=1, keepdims=True)
    token_total = jnp.sum(jnp.where(lane == 64, everything, 0.0), axis=1, keepdims=True)
    loss_total = jnp.sum(jnp.where(lane == 65, everything, 0.0), axis=1, keepdims=True)
    grad_norm = jnp.sqrt(square_total) / token_total
    clip_factor = jnp.minimum(1.0, MAX_NORM / (grad_norm + 1e-06))
    scalars[...] = jnp.where(lane == 0, grad_norm, loss_total / token_total)
    kept = [states[n].reshape(GROUPS, 8, 128) for n in range(3)]
    for g in range(GROUPS):
        clipped = totals[g] / token_total * clip_factor
        weight, first, second = kept[0][g], kept[1][g], kept[2][g]
        first = BETA_FIRST * first + (1.0 - BETA_FIRST) * clipped
        second = BETA_SECOND * second + (1.0 - BETA_SECOND) * clipped * clipped
        update = (first * first_scale) / (jnp.sqrt(second * second_scale) + EPSILON_ADAM) + DECAY_RATE * weight
        new_first[g] = first
        new_second[g] = second
        adam[g] = update
        new_weight[g] = weight - LEARN_RATE * update

    for k in range(CHUNKS):
        for copies in (to_core, to_opp, to_dir, to_mer):
            copies[k].wait_send()
    for g in range(GROUPS):
        wait_bytes(y_in.at[g], y_send.at[g])
        wait_bytes(z_in.at[g, pl.ds(0, Z - 1)], z_send.at[g])
    wait_bytes(pair_in.at[pl.ds(0, Z - 1)], pair_send)
    wait_bytes(notes_in.at[pl.ds(0, PLANE - 1)], note_send)


def in_tiles(array):
    return array.reshape(2, TILES, 128).transpose(1, 0, 2)


def in_rows(array):
    return array.reshape(TILES, 2, 128).transpose(1, 0, 2).reshape(2, WIDTH)


def on_device(
    small_cols, wide_cols, token_counts, loss_sums, weight, first_moment, second_moment, step
):
    vmem, dma = pltpu.VMEM, pltpu.SemaphoreType.DMA
    block = jax.ShapeDtypeStruct((GROUPS, 8, 128), F32)
    *arrays, scalars = pl.pallas_call(
        kernel,
        name="reduce_and_step",
        out_shape=[block] * 4 + [jax.ShapeDtypeStruct((1, 128), F32)],
        in_specs=[pl.BlockSpec(memory_space=pl.ANY)] * 8,
        out_specs=[pl.BlockSpec(memory_space=pltpu.VMEM)] * 5,
        scratch_shapes=[
            vmem((TOKENS, ROWS), BF16),
            vmem((TILES, TOKENS, 2, 128), BF16),
            vmem((ROWS, 2 * TOKENS), BF16),
            vmem((CHUNKS, 2, X, 16, 256), F32),
            vmem((CHUNKS, X, 16, 256), F32),
            vmem((CHUNKS, X, 16, 256), F32),
            vmem((CHUNKS, 16, 256), F32),
            vmem((CHUNKS, 16, 256), F32),
            vmem((CHUNKS, 16, 256), F32),
            vmem((CHUNKS, 16, 256), F32),
            vmem((GROUPS, 8 * Y, 128), F32),
            vmem((GROUPS, Y - 1, 8, 128), F32),
            vmem((GROUPS, 8, 128), F32),
            vmem((GROUPS, Z, 8, 128), F32),
            vmem((1, 128), F32),
            vmem((Z, 1, 128), F32),
            vmem((1, 128), F32),
            vmem((PLANE, 1, 128), F32),
            vmem((3, TILES, 2, 128), F32),
            pltpu.SMEM((1,), jnp.int32),
            pltpu.SMEM((1,), F32),
            pltpu.SMEM((1,), jnp.int32),
            dma((4,)),
            dma((TILES,)),
            dma((3,)),
        ]
        + [dma((CHUNKS,))] * 8
        + [dma((GROUPS,))] * 4
        + [dma(())] * 4
        + [pltpu.SemaphoreType.REGULAR((3,))],
        compiler_params=pltpu.CompilerParams(
            collective_id=0, has_side_effects=True, vmem_limit_bytes=67_043_328
        ),
    )(
        small_cols, wide_cols, token_counts, loss_sums,
        in_tiles(weight), in_tiles(first_moment), in_tiles(second_moment), step.reshape(1),
    )
    new_weight, new_first, new_second, adam = (in_rows(a) for a in arrays)
    return (new_weight, new_first, new_second, adam, scalars[0, 0], scalars[0, 1])


def solution(mesh):
    in_specs = (
        P(("dp", "fsdp"), None),
        P(("dp", "fsdp"), None, None),
        P(("dp", "fsdp")),
        P(("dp", "fsdp")),
        P("fsdp", None),
        P("fsdp", None),
        P("fsdp", None),
        P(),
    )
    out_specs = (P("fsdp", None), P("fsdp", None), P("fsdp", None), P("fsdp", None), P(), P())
    return jax.shard_map(
        on_device, mesh=mesh, in_specs=in_specs, out_specs=out_specs, check_vma=False
    )
```

time: 85.8 us -> 50.8 us (0.59)
  Pallas kernels: 0 us -> 42.5 us
  waiting for transfers between devices: 31 us -> 0 us
  starting transfers between devices: 18.9 us -> 0 us
  blocking collectives: 17.5 us -> 0 us
  between operations: 7.79 us -> 2.58 us
  matrix products: 3.28 us -> 0 us
  other arithmetic: 3.08 us -> 0 us
  local copies, waits for them, and re-layouts: 3.8 us -> 5.32 us
    pallas_call x0 -> x1, Pallas kernels: none -> 42.5 us  [on_device(): pl.pallas_call(kernel, name='reduce_and_step', out_shape=[block] * 4 + [j...]
    all_to_all x2 -> x0, waiting for transfers between devices: 31 us -> none  [the longest x1 22.4 us: sum_at_owner(): parts = lax.all_to_all(in_blocks(array, dim, peers), axis, 0, 0, tiled=True)]
    all_to_all x2 -> x0, starting transfers between devices: 18.9 us -> none  [the longest x1 11.6 us: sum_at_owner(): parts = lax.all_to_all(in_blocks(array, dim, peers), axis, 0, 0, tiled=True)]
    all_to_all x1 -> x0, blocking collectives: 17.5 us -> none  [from_everyone(): lax.all_to_all(jnp.broadcast_to(array[None], (peers, *array.shape)), axis...]
    reshape x1 -> x6, local copies, waits for them, and re-layouts: 0.02 us -> 4.06 us  [in_rows(): return array.reshape(TILES, 2, 128).transpose(1, 0, 2).reshape(2, WIDTH)]
    dot_general x1 -> x0, matrix products: 3.28 us -> none  [slot_product(): jnp.einsum('thc,thd->hcd', narrow.reshape(block_rows, 2, half_cols), broa...]
    another operation x1 -> x0, local copies, waits for them, and re-layouts: 1.34 us -> none  [in_blocks(): array.reshape(*lengths[:dim], peers, lengths[dim] // peers, *lengths[dim...]
    unnamed x7 -> x0, local copies, waits for them, and re-layouts: 1.08 us -> none
  transfers between devices with their start and end apart: 2 -> 0, of which waited for: 2 -> 0; matrix products, arithmetic and copies ran while one was open for 0% -> 0% of each run, Pallas kernels for 0% -> 0%
where the time goes in v1:
time: 50.8 us; the launch traced here: 50.4 us
  Pallas kernels  42.5 us (84%)
  local copies, waits for them, and re-layouts  5.32 us (10%)
  between operations  2.58 us (5%)
    pallas_call x1, Pallas kernels, on_device(): pl.pallas_call(kernel, name='reduce_and_step', out_shape=[block] * 4 + [j...  42.5 us
    reshape x6, local copies, waits for them, and re-layouts, in_rows(): return array.reshape(TILES, 2, 128).transpose(1, 0, 2).reshape(2, WIDTH)  4.06 us
    slice x1, local copies, waits for them, and re-layouts, on_device(): scalars[0, 1]  1.25 us

profile of v1, /device:TPU:1, one launch (start us, length us, event | category | flops | bytes accessed | tf_op | source)
XLA Modules:
  0.0 50.4 jit_solution(13568751693851658915)
XLA Ops:
  2.6 42.5 %reduce_and_step.1 = (f32[3,8,128]{2,1,0:T(8,128)}, f32[3,8,128]{2,1,0:T(8,128)}, f32[3,8,128]{2,1,0:T(8,128)}, f32[3,8,128]{2,1,0:T(8,128)}, f32[1,128]{1,0:T(1,128)}) custom-call(bf16[768,128]{1,0:T(8,128)(2,1)} %small_hbm.1, bf16[768,2,1536]{2,1,0:T(2,128)(2,1)} %wide_hbm.1, s32[1]{0:T(128)S(6)} %copy.38.count_hbm, f32[1]{0:T(128)S(6)} %copy.39.loss_hbm, ...), custom_call_target="tpu_custom_call" | custom-call | tf_op jit(solution)/shard_map/reduce_and_step/pallas_call | solution.py:296
  45.1 0.7 %copy.34 = f32[12,2,128]{2,0,1:T(8,128)S(1)} copy(f32[12,2,128]{2,1,0:T(2,128)} %bitcast.51) | data formatting | bytes 24576 | tf_op jit(solution)/shard_map/reshape | solution.py:288
  45.8 0.7 %copy.35 = f32[12,2,128]{2,0,1:T(8,128)S(1)} copy(f32[12,2,128]{2,1,0:T(2,128)} %bitcast.50) | data formatting | bytes 24576 | tf_op jit(solution)/shard_map/reshape | solution.py:288
  46.5 0.6 %copy_bitcast_fusion.4 = (f32[2,1536]{1,0:T(2,128)}, f32[2,1536]{1,0:T(2,128)}) fusion(f32[1,2,12,128]{3,2,1,0:T(8,128)S(1)} %bitcast.41, f32[1,2,12,128]{3,2,1,0:T(8,128)S(1)} %bitcast.43), kind=kLoop, calls=%fused_computation.4 | loop fusion | bytes 49152 | tf_op jit(solution)/shard_map/reshape | solution.py:288
  47.1 0.7 %copy.36 = f32[12,2,128]{2,0,1:T(8,128)S(1)} copy(f32[12,2,128]{2,1,0:T(2,128)} %bitcast.49) | data formatting | bytes 24576 | tf_op jit(solution)/shard_map/reshape | solution.py:288
  47.8 0.7 %copy.37 = f32[12,2,128]{2,0,1:T(8,128)S(1)} copy(f32[12,2,128]{2,1,0:T(2,128)} %bitcast.48) | data formatting | bytes 24576 | tf_op jit(solution)/shard_map/reshape | solution.py:288
  48.5 0.6 %copy_bitcast_fusion.6 = (f32[2,1536]{1,0:T(2,128)}, f32[2,1536]{1,0:T(2,128)}) fusion(f32[1,2,12,128]{3,2,1,0:T(8,128)S(1)} %bitcast.42, f32[1,2,12,128]{3,2,1,0:T(8,128)S(1)} %bitcast.44), kind=kLoop, calls=%fused_computation.6 | loop fusion | bytes 49152 | tf_op jit(solution)/shard_map/reshape | solution.py:288
  49.1 1.3 %fusion = (f32[1,1]{1,0:T(1,128)}, f32[1,1]{1,0:T(1,128)}) fusion(f32[1,128]{1,0:T(1,128)} %get-tuple-element.15), kind=kLoop, calls=%fused_computation.8 | loop fusion | bytes 16 | tf_op jit(solution)/shard_map/slice | solution.py:341
